TPU v7x, 32 devices: a whole 2x2x4 slice. The times are simulated.
32 devices in a mesh: grp: 4 (over y, x), section: 2 (over core), row: 4 (over z).
Axes of the slice: x: 2, y: 2, z: 4, core: 2. Of those that a mesh axis runs over, the one named last changes fastest.
Arguments:
- matrices: float32 [4, 8192, 8192], P('grp', 'row', 'section'), parts along dimension 0, may hold values from -57 to 57, as said below
Outputs:
- reduced: float32 [4, 8192, 8192], P('grp', 'row', 'section'), parts along dimension 0
There are 4 independent parts, one for each index of `grp`. A program takes and returns all parts, laid end to end along the dimension named above; each array names one. Nothing has to cross between parts.
Inputs may be any that keep to these rules, and one draw needn't show every extreme that they name: `matrices`: each matrix is exactly symmetric.
All inputs are finite; a program needn't handle non-finite values.
Results may differ from a plain program's by a relative error of at most 0.00023.
Values sent between devices are 32-bit elements; how exact they have to be, the bound alone decides.
No kernel may reach another device: no remote copies, remote signals or barrier semaphores. Data moves between devices by JAX's collectives and lax.ppermute only.
A program may use at most 128 MiB of HBM per device.

v0:
```python
import jax
import jax.numpy as jnp
from jax import lax
from jax.sharding import PartitionSpec as P

NB = 8
highest = lax.Precision.HIGHEST


def broadcast(value, axis, source):
    kept = jnp.where(lax.axis_index(axis) == source, value, 0).astype(value.dtype)
    return lax.psum(kept, axis)


def local(matrices):
    height = matrices.shape[1]
    breadth = matrices.shape[2]
    order = height * lax.axis_size("row")
    row_start = lax.axis_index("row") * height
    col_start = lax.axis_index("section") * breadth
    owned = jnp.swapaxes(matrices[:, :, :NB], 1, 2)
    owned = broadcast(owned, "section", 0)
    panel_cols = lax.all_gather(owned, "row", axis=2, tiled=True)
    positions = jnp.arange(order, dtype=jnp.int32)
    left_list = []
    right_list = []
    for column in range(NB):
        current = panel_cols[:, column, :]
        if column > 0:
            lefts = jnp.stack(left_list, 1)
            rights = jnp.stack(right_list, 1)
            current = current - jnp.einsum(
                "mkn,mk->mn", lefts, rights[:, :, column], precision=highest
            )
            current = current - jnp.einsum(
                "mkn,mk->mn", rights, lefts[:, :, column], precision=highest
            )
        below = jnp.where(positions[None, :] > column, current, 0.0)
        length = jnp.sqrt(jnp.sum(below * below, axis=1))
        reflector = below + jnp.where(positions[None, :] == column + 1, length[:, None], 0.0)
        scaling = 2.0 / (jnp.sum(reflector * reflector, axis=1) + 1e-06)
        row_part = lax.dynamic_slice_in_dim(reflector, row_start, height, 1)
        partial_cols = jnp.einsum("mij,mi->mj", matrices, row_part, precision=highest)
        summed_cols = lax.psum(partial_cols, "row")
        image = lax.all_gather(summed_cols, "section", axis=1, tiled=True)
        if column > 0:
            right_dots = jnp.einsum("mkn,mn->mk", rights, reflector, precision=highest)
            left_dots = jnp.einsum("mkn,mn->mk", lefts, reflector, precision=highest)
            image = image - jnp.einsum("mkn,mk->mn", lefts, right_dots, precision=highest)
            image = image - jnp.einsum("mkn,mk->mn", rights, left_dots, precision=highest)
        corrected = scaling[:, None] * image
        inner = jnp.sum(corrected * reflector, axis=1)
        partner = corrected - (0.5 * scaling * inner)[:, None] * reflector
        left_list.append(reflector)
        right_list.append(partner)
    lefts = jnp.stack(left_list, 1)
    rights = jnp.stack(right_list, 1)
    rows_left = lax.dynamic_slice_in_dim(lefts, row_start, height, 2)
    rows_right = lax.dynamic_slice_in_dim(rights, row_start, height, 2)
    cols_left = lax.dynamic_slice_in_dim(lefts, col_start, breadth, 2)
    cols_right = lax.dynamic_slice_in_dim(rights, col_start, breadth, 2)
    reduced = matrices - jnp.einsum("mki,mkj->mij", rows_left, cols_right, precision=highest)
    reduced = reduced - jnp.einsum("mki,mkj->mij", rows_right, cols_left, precision=highest)
    return reduced


def solution(mesh):
    in_specs = (P("grp", "row", "section"),)
    out_specs = P("grp", "row", "section")
    return jax.shard_map(local, mesh=mesh, in_specs=in_specs, out_specs=out_specs, check_vma=False)
```

profile of v0, /device:TPU:0, one launch (start us, length us, event | category | flops | bytes accessed | tf_op | source)
XLA Modules:
  0.0 484.6 jit_solution(7150372267628386064)
XLA Ops:
  6.5 1.3 slice.69
  8.1 0.6 select_bitcast_fusion
  8.8 21.3 %all-reduce.2.cloned.1.call-done = f32[1,8,2048]{2,1,0:T(8,128)} async-done(((f32[1,8,2048]{2,1,0:T(8,128)}), f32[1,8,2048]{2,1,0:T(8,128)}) %all-reduce.2.cloned.1.call-update) | async-done | bytes 65552 | tf_op jit(solution)/shard_map/psum | solution.py:12
  30.1 14.4 %all_gather.27 = f32[1,8,8192]{2,1,0:T(8,128)S(1)} all-gather(f32[1,8,2048]{2,1,0:T(8,128)} %all-reduce.2.cloned.1.call-done), channel_id=1, replica_groups=mesh['grp'=4,'section'=2,'row'=4] {'row'}, dimensions={2}, use_global_device_ids=true | all-gather | bytes 327680 | tf_op jit(solution)/shard_map/all_gather | solution.py:23
  44.5 0.7 multiply_reduce_fusion.25
  45.9 0.7 multiply_reduce_fusion.24
  46.8 0.7 slice.95
  47.4 19.5 %fusion.14 = f32[1,4096]{1,0:T(1,128)S(1)} fusion(f32[1,2048,4096]{2,1,0:T(8,128)} %param.1, f32[1,8192]{1,0:T(1,128)S(1)} %get-tuple-element.26, s32[]{:T(128)S(6)} %select_n.146), kind=kOutput, calls=%fused_computation.16 | convolution fusion | flops 100663296 | bytes 33579012 | tf_op jit(solution)/shard_map/mij,mi->mj/dot_general | solution.py:43
  66.9 19.3 %psum.64 = f32[1,4096]{1,0:T(1,128)S(1)} all-reduce(f32[1,4096]{1,0:T(1,128)S(1)} %fusion.14), channel_id=1, replica_groups=mesh['grp'=4,'section'=2,'row'=4] {'row'}, use_global_device_ids=true, to_apply=%region_3.4 | all-reduce | flops 4096 | bytes 32768 | tf_op jit(solution)/shard_map/psum | solution.py:44
  86.2 1.8 all_gather.28
  88.7 0.7 multiply_reduce_fusion.23
  90.6 1.9 multiply_reduce_fusion.22
  93.2 0.7 multiply_reduce_fusion.21
  94.8 19.5 %fusion.12 = f32[1,4096]{1,0:T(1,128)S(1)} fusion(f32[2048,1]{0,1:T(1,128)S(1)} %bitcast.471, f32[1,2048,4096]{2,1,0:T(8,128)} %param.1), kind=kOutput, calls=%fused_computation.14 | convolution fusion | flops 100663296 | bytes 33579008 | tf_op jit(solution)/shard_map/mij,mi->mj/dot_general | solution.py:43
  114.3 15.5 %psum.65 = f32[1,4096]{1,0:T(1,128)S(1)} all-reduce(f32[1,4096]{1,0:T(1,128)S(1)} %fusion.12), channel_id=1, replica_groups=mesh['grp'=4,'section'=2,'row'=4] {'row'}, use_global_device_ids=true, to_apply=%region_7.8 | all-reduce | flops 4096 | bytes 32768 | tf_op jit(solution)/shard_map/psum | solution.py:44
  129.8 2.1 all_gather.29
  131.9 1.3 broadcast_multiply_fusion.7
  133.2 0.7 multiply_reduce_fusion.20
  135.6 0.6 multiply_reduce_fusion.19
  136.9 0.6 multiply_reduce_fusion.18
  137.5 0.7 convolution_bitcast_fusion.10
  138.1 0.7 convolution_bitcast_fusion.11
  139.5 19.5 %fusion.10 = f32[1,4096]{1,0:T(1,128)S(1)} fusion(f32[2048,1]{0,1:T(1,128)S(1)} %bitcast.466, f32[1,2048,4096]{2,1,0:T(8,128)} %param.1), kind=kOutput, calls=%fused_computation.12 | convolution fusion | flops 100663296 | bytes 33579008 | tf_op jit(solution)/shard_map/mij,mi->mj/dot_general | solution.py:43
  159.1 16.3 %psum.66 = f32[1,4096]{1,0:T(1,128)S(1)} all-reduce(f32[1,4096]{1,0:T(1,128)S(1)} %fusion.10), channel_id=1, replica_groups=mesh['grp'=4,'section'=2,'row'=4] {'row'}, use_global_device_ids=true, to_apply=%region_11.12 | all-reduce | flops 4096 | bytes 32768 | tf_op jit(solution)/shard_map/psum | solution.py:44
  175.3 2.3 all_gather.30
  178.1 1.0 multiply_reduce_fusion.17
  182.6 0.6 multiply_reduce_fusion.15
  183.2 0.7 convolution_bitcast_fusion.8
  183.9 0.7 convolution_bitcast_fusion.9
  185.3 19.5 %fusion.8 = f32[1,4096]{1,0:T(1,128)S(1)} fusion(f32[2048,1]{0,1:T(1,128)S(1)} %bitcast.467, f32[1,2048,4096]{2,1,0:T(8,128)} %param.1), kind=kOutput, calls=%fused_computation.10 | convolution fusion | flops 100663296 | bytes 33579008 | tf_op jit(solution)/shard_map/mij,mi->mj/dot_general | solution.py:43
  204.8 15.6 %psum.67 = f32[1,4096]{1,0:T(1,128)S(1)} all-reduce(f32[1,4096]{1,0:T(1,128)S(1)} %fusion.8), channel_id=1, replica_groups=mesh['grp'=4,'section'=2,'row'=4] {'row'}, use_global_device_ids=true, to_apply=%region_15.16 | all-reduce | flops 4096 | bytes 32768 | tf_op jit(solution)/shard_map/psum | solution.py:44
  220.3 2.0 all_gather.31
  222.8 1.1 multiply_reduce_fusion.14
  227.2 0.6 multiply_reduce_fusion.12
  227.8 0.7 convolution_bitcast_fusion.6
  228.5 0.7 convolution_bitcast_fusion.7
  229.9 19.5 %fusion.6 = f32[1,4096]{1,0:T(1,128)S(1)} fusion(f32[2048,1]{0,1:T(1,128)S(1)} %bitcast.468, f32[1,2048,4096]{2,1,0:T(8,128)} %param.1), kind=kOutput, calls=%fused_computation.8 | convolution fusion | flops 100663296 | bytes 33579008 | tf_op jit(solution)/shard_map/mij,mi->mj/dot_general | solution.py:43
  249.4 16.3 %psum.68 = f32[1,4096]{1,0:T(1,128)S(1)} all-reduce(f32[1,4096]{1,0:T(1,128)S(1)} %fusion.6), channel_id=1, replica_groups=mesh['grp'=4,'section'=2,'row'=4] {'row'}, use_global_device_ids=true, to_apply=%region_19.20 | all-reduce | flops 4096 | bytes 32768 | tf_op jit(solution)/shard_map/psum | solution.py:44
  265.7 2.0 all_gather.32
  268.0 1.0 multiply_reduce_fusion.11
  272.6 0.6 multiply_reduce_fusion.9
  273.2 0.7 convolution_bitcast_fusion.4
  273.9 0.7 convolution_bitcast_fusion.5
  275.3 19.5 %fusion.4 = f32[1,4096]{1,0:T(1,128)S(1)} fusion(f32[2048,1]{0,1:T(1,128)S(1)} %bitcast.469, f32[1,2048,4096]{2,1,0:T(8,128)} %param.1), kind=kOutput, calls=%fused_computation.6 | convolution fusion | flops 100663296 | bytes 33579008 | tf_op jit(solution)/shard_map/mij,mi->mj/dot_general | solution.py:43
  294.8 15.6 %psum.69 = f32[1,4096]{1,0:T(1,128)S(1)} all-reduce(f32[1,4096]{1,0:T(1,128)S(1)} %fusion.4), channel_id=1, replica_groups=mesh['grp'=4,'section'=2,'row'=4] {'row'}, use_global_device_ids=true, to_apply=%region_23.24 | all-reduce | flops 4096 | bytes 32768 | tf_op jit(solution)/shard_map/psum | solution.py:44
  310.4 2.1 all_gather.33
  312.8 1.0 multiply_reduce_fusion.8
  317.5 0.6 multiply_reduce_fusion.6
  318.1 0.7 convolution_bitcast_fusion.2
  318.8 0.7 convolution_bitcast_fusion.3
  320.2 19.5 %fusion.2 = f32[1,4096]{1,0:T(1,128)S(1)} fusion(f32[2048,1]{0,1:T(1,128)S(1)} %bitcast.470, f32[1,2048,4096]{2,1,0:T(8,128)} %param.1), kind=kOutput, calls=%fused_computation.4 | convolution fusion | flops 100663296 | bytes 33579008 | tf_op jit(solution)/shard_map/mij,mi->mj/dot_general | solution.py:43
  339.7 16.2 %psum.70 = f32[1,4096]{1,0:T(1,128)S(1)} all-reduce(f32[1,4096]{1,0:T(1,128)S(1)} %fusion.2), channel_id=1, replica_groups=mesh['grp'=4,'section'=2,'row'=4] {'row'}, use_global_device_ids=true, to_apply=%region_27.28 | all-reduce | flops 4096 | bytes 32768 | tf_op jit(solution)/shard_map/psum | solution.py:44
  355.9 2.3 all_gather.34
  358.5 1.0 multiply_reduce_fusion.5
  362.0 0.6 multiply_reduce_fusion.4
  363.3 0.6 multiply_reduce_fusion.3
  363.9 0.7 convolution_bitcast_fusion
  364.6 0.7 convolution_bitcast_fusion.1
  366.0 19.5 %fusion = f32[1,4096]{1,0:T(1,128)S(1)} fusion(f32[2048,1]{0,1:T(1,128)S(1)} %bitcast.465, f32[1,2048,4096]{2,1,0:T(8,128)} %param.1), kind=kOutput, calls=%fused_computation.2 | convolution fusion | flops 100663296 | bytes 33579008 | tf_op jit(solution)/shard_map/mij,mi->mj/dot_general | solution.py:43
  385.5 15.6 %psum.71 = f32[1,4096]{1,0:T(1,128)S(1)} all-reduce(f32[1,4096]{1,0:T(1,128)S(1)} %fusion), channel_id=1, replica_groups=mesh['grp'=4,'section'=2,'row'=4] {'row'}, use_global_device_ids=true, to_apply=%region_31.32 | all-reduce | flops 4096 | bytes 32768 | tf_op jit(solution)/shard_map/psum | solution.py:44
  401.1 2.0 all_gather.35
  403.4 1.0 multiply_reduce_fusion.2
  405.9 30.3 %fusion.47 = f32[2048,4096]{1,0:T(8,128)} fusion(f32[1,8,8192]{2,1,0:T(8,128)S(1)} %stack.172, s32[]{:T(128)S(6)} %select_n.161, f32[1,8,8192]{2,1,0:T(8,128)S(1)} %stack.84, s32[]{:T(128)S(6)} %select_n.146), kind=kOutput, calls=%fused_computation.77 | convolution fusion | flops 805306368 | bytes 33751048 | tf_op jit(solution)/shard_map/mki,mkj->mij/dot_general | solution.py:62
  436.3 41.3 %bitcast_subtract_fusion = f32[1,2048,4096]{2,1,0:T(8,128)} fusion(f32[1,2048,4096]{2,1,0:T(8,128)} %param.1, f32[2048,4096]{1,0:T(8,128)} %fusion.47, f32[1,8,8192]{2,1,0:T(8,128)S(1)} %stack.84, s32[]{:T(128)S(6)} %select_n.161, f32[1,8,8192]{2,1,0:T(8,128)S(1)} %stack.172, s32[]{:T(128)S(6)} %select_n.146), kind=kOutput, calls=%fused_computation | convolution fusion | flops 822083584 | bytes 100859912 | tf_op jit(solution)/shard_map/mki,mkj->mij/dot_general | solution.py:63
  (73 shorter events, 15.7 us)
Async XLA Ops:
  6.5 23.6 %all-reduce.2.cloned.1.call-start = ((), (), s32[]{:S(2)}) async-start(), calls=%async_computation | async-start | bytes 131072 | tf_op jit(solution)/shard_map/psum | solution.py:12
Sparse Core Ops, SparseCore 0:
  9.6 20.4 all-reduce.1
where the time goes:
time: 492 us; the launch traced here: 485 us
  matrix products  249 us (51%)
  blocking collectives  161 us (33%)
  between operations  30.3 us (6%)
  waiting for transfers between devices  21.3 us (4%)
  other arithmetic  15.9 us (3%)
  local copies, waits for them, and re-layouts  7.2 us (1%)
    dot_general x8, matrix products, local(): jnp.einsum('mij,mi->mj', matrices, row_part, precision=highest)  156 us
    psum x8, blocking collectives, local(): summed_cols = lax.psum(partial_cols, 'row')  130 us
    dot_general x1, matrix products, local(): jnp.einsum('mki,mkj->mij', rows_right, cols_left, precision=highest)  41.3 us
    dot_general x1, matrix products, local(): jnp.einsum('mki,mkj->mij', rows_left, cols_right, precision=highest)  30.3 us
    psum x1, waiting for transfers between devices, broadcast(): return lax.psum(kept, axis)  21.3 us
    all_gather x8, blocking collectives, local(): image = lax.all_gather(summed_cols, 'section', axis=1, tiled=True)  16.6 us
    all_gather x1, blocking collectives, local(): panel_cols = lax.all_gather(owned, 'row', axis=2, tiled=True)  14.4 us
  transfers between devices with their start and end apart: 1, of which 1 were waited for; matrix products, arithmetic and copies ran while one was open for 0% of the time, Pallas kernels for 0%

commit v1 on v0

--- a/solution.py
+++ b/solution.py
@@ -41,7 +41,8 @@
         scaling = 2.0 / (jnp.sum(reflector * reflector, axis=1) + 1e-06)
         row_part = lax.dynamic_slice_in_dim(reflector, row_start, height, 1)
         partial_cols = jnp.einsum("mij,mi->mj", matrices, row_part, precision=highest)
-        summed_cols = lax.psum(partial_cols, "row")
+        blocks = lax.all_gather(partial_cols, "row", axis=0, tiled=False)
+        summed_cols = blocks.sum(axis=0)
         image = lax.all_gather(summed_cols, "section", axis=1, tiled=True)
         if column > 0:
             right_dots = jnp.einsum("mkn,mn->mk", rights, reflector, precision=highest)

time: 492 us -> 467 us (0.949)
  blocking collectives: 161 us -> 136 us
    psum x8 -> x0, blocking collectives: 130 us -> none  [local(): summed_cols = lax.psum(partial_cols, 'row')]
    all_gather x0 -> x8, blocking collectives: none -> 105 us  [local(): blocks = lax.all_gather(partial_cols, 'row', axis=0, tiled=False)]
where the time goes in v1:
time: 467 us; the launch traced here: 460 us
  matrix products  245 us (52%)
  blocking collectives  136 us (29%)
  between operations  30.6 us (7%)
  waiting for transfers between devices  21.3 us (5%)
  other arithmetic  19.6 us (4%)
  local copies, waits for them, and re-layouts  7.41 us (2%)
    dot_general x8, matrix products, local(): jnp.einsum('mij,mi->mj', matrices, row_part, precision=highest)  156 us
    all_gather x8, blocking collectives, local(): blocks = lax.all_gather(partial_cols, 'row', axis=0, tiled=False)  105 us
    dot_general x1, matrix products, local(): jnp.einsum('mki,mkj->mij', rows_right, cols_left, precision=highest)  41.4 us
    dot_general x1, matrix products, local(): jnp.einsum('mki,mkj->mij', rows_left, cols_right, precision=highest)  30.3 us
    psum x1, waiting for transfers between devices, broadcast(): return lax.psum(kept, axis)  21.3 us
    all_gather x8, blocking collectives, local(): image = lax.all_gather(summed_cols, 'section', axis=1, tiled=True)  16.5 us
    all_gather x1, blocking collectives, local(): panel_cols = lax.all_gather(owned, 'row', axis=2, tiled=True)  14.4 us
  transfers between devices with their start and end apart: 1, of which 1 were waited for; matrix products, arithmetic and copies ran while one was open for 0% of the time, Pallas kernels for 0%

profile of v1, /device:TPU:0, one launch (start us, length us, event | category | flops | bytes accessed | tf_op | source)
XLA Modules:
  0.0 460.1 jit_solution(17159064692361487187)
XLA Ops:
  6.5 1.3 slice.69
  8.1 0.6 select_bitcast_fusion
  8.8 21.3 %all-reduce.2.cloned.1.call-done = f32[1,8,2048]{2,1,0:T(8,128)} async-done(((f32[1,8,2048]{2,1,0:T(8,128)}), f32[1,8,2048]{2,1,0:T(8,128)}) %all-reduce.2.cloned.1.call-update) | async-done | bytes 65552 | tf_op jit(solution)/shard_map/psum | solution.py:12
  30.1 14.4 %all_gather.75 = f32[1,8,8192]{2,1,0:T(8,128)S(1)} all-gather(f32[1,8,2048]{2,1,0:T(8,128)} %all-reduce.2.cloned.1.call-done), channel_id=1, replica_groups=mesh['grp'=4,'section'=2,'row'=4] {'row'}, dimensions={2}, use_global_device_ids=true | all-gather | bytes 327680 | tf_op jit(solution)/shard_map/all_gather | solution.py:23
  44.5 0.7 multiply_reduce_fusion.25
  45.9 0.7 multiply_reduce_fusion.24
  46.8 0.7 slice.95
  47.4 19.5 %fusion.14 = f32[1,4096]{1,0:T(1,128)S(1)} fusion(f32[1,2048,4096]{2,1,0:T(8,128)} %param.1, f32[1,8192]{1,0:T(1,128)S(1)} %get-tuple-element.38, s32[]{:T(128)S(6)} %select_n.146), kind=kOutput, calls=%fused_computation.16 | convolution fusion | flops 100663296 | bytes 33579012 | tf_op jit(solution)/shard_map/mij,mi->mj/dot_general | solution.py:43
  66.9 13.2 %all-gather = f32[16384]{0:T(1024)S(1)} all-gather(f32[4096]{0:T(1024)S(1)} %bitcast.469), channel_id=2, replica_groups=mesh['grp'=4,'section'=2,'row'=4] {'row'}, dimensions={0}, use_global_device_ids=true | all-gather | bytes 81920 | tf_op jit(solution)/shard_map/all_gather | solution.py:44
  80.2 1.8 all-gather.1
  82.7 0.7 multiply_reduce_fusion.23
  84.7 1.9 multiply_reduce_fusion.22
  87.2 0.7 multiply_reduce_fusion.1
  88.7 19.5 %fusion.12 = f32[1,4096]{1,0:T(1,128)S(1)} fusion(f32[2048,1]{0,1:T(1,128)S(1)} %bitcast.476, f32[1,2048,4096]{2,1,0:T(8,128)} %param.1), kind=kOutput, calls=%fused_computation.14 | convolution fusion | flops 100663296 | bytes 33579008 | tf_op jit(solution)/shard_map/mij,mi->mj/dot_general | solution.py:43
  108.2 13.2 %all-gather.2 = f32[16384]{0:T(1024)S(1)} all-gather(f32[4096]{0:T(1024)S(1)} %bitcast.465), channel_id=4, replica_groups=mesh['grp'=4,'section'=2,'row'=4] {'row'}, dimensions={0}, use_global_device_ids=true | all-gather | bytes 81920 | tf_op jit(solution)/shard_map/all_gather | solution.py:44
  121.5 2.0 all-gather.3
  123.6 1.9 multiply_reduce_fusion.8
  127.1 0.6 multiply_reduce_fusion.20
  128.4 0.6 multiply_reduce_fusion.19
  129.0 0.7 convolution_bitcast_fusion.10
  129.7 0.7 convolution_bitcast_fusion.11
  131.1 19.5 %fusion.10 = f32[1,4096]{1,0:T(1,128)S(1)} fusion(f32[2048,1]{0,1:T(1,128)S(1)} %bitcast.474, f32[1,2048,4096]{2,1,0:T(8,128)} %param.1), kind=kOutput, calls=%fused_computation.12 | convolution fusion | flops 100663296 | bytes 33579008 | tf_op jit(solution)/shard_map/mij,mi->mj/dot_general | solution.py:43
  151.4 13.2 %all-gather.4 = f32[16384]{0:T(1024)S(1)} all-gather(f32[4096]{0:T(1024)S(1)} %bitcast.463), channel_id=6, replica_groups=mesh['grp'=4,'section'=2,'row'=4] {'row'}, dimensions={0}, use_global_device_ids=true | all-gather | bytes 81920 | tf_op jit(solution)/shard_map/all_gather | solution.py:44
  164.6 2.1 all-gather.5
  169.4 0.6 multiply_reduce_fusion.18
  170.8 0.6 multiply_reduce_fusion.17
  171.4 0.7 convolution_bitcast_fusion.8
  172.0 0.7 convolution_bitcast_fusion.9
  173.4 19.5 %fusion.8 = f32[1,4096]{1,0:T(1,128)S(1)} fusion(f32[2048,1]{0,1:T(1,128)S(1)} %bitcast.475, f32[1,2048,4096]{2,1,0:T(8,128)} %param.1), kind=kOutput, calls=%fused_computation.10 | convolution fusion | flops 100663296 | bytes 33579008 | tf_op jit(solution)/shard_map/mij,mi->mj/dot_general | solution.py:43
  193.8 13.2 %all-gather.6 = f32[16384]{0:T(1024)S(1)} all-gather(f32[4096]{0:T(1024)S(1)} %bitcast.464), channel_id=8, replica_groups=mesh['grp'=4,'section'=2,'row'=4] {'row'}, dimensions={0}, use_global_device_ids=true | all-gather | bytes 81920 | tf_op jit(solution)/shard_map/all_gather | solution.py:44
  207.1 2.3 all-gather.7
  209.4 0.6 multiply_reduce_fusion.6
  212.0 0.6 multiply_reduce_fusion.16
  213.3 0.6 multiply_reduce_fusion.15
  213.9 0.7 convolution_bitcast_fusion.6
  214.6 0.7 convolution_bitcast_fusion.7
  216.7 19.5 %fusion.6 = f32[1,4096]{1,0:T(1,128)S(1)} fusion(f32[2048,1]{0,1:T(1,128)S(1)} %bitcast.471, f32[1,2048,4096]{2,1,0:T(8,128)} %param.1), kind=kOutput, calls=%fused_computation.8 | convolution fusion | flops 100663296 | bytes 33579008 | tf_op jit(solution)/shard_map/mij,mi->mj/dot_general | solution.py:43
  236.2 13.1 %all-gather.8 = f32[16384]{0:T(1024)S(1)} all-gather(f32[4096]{0:T(1024)S(1)} %bitcast.466), channel_id=10, replica_groups=mesh['grp'=4,'section'=2,'row'=4] {'row'}, dimensions={0}, use_global_device_ids=true | all-gather | bytes 81920 | tf_op jit(solution)/shard_map/all_gather | solution.py:44
  249.4 2.0 all-gather.9
  251.4 0.6 multiply_reduce_fusion.5
  254.3 0.6 multiply_reduce_fusion.14
  255.6 0.6 multiply_reduce_fusion.13
  256.2 0.7 convolution_bitcast_fusion.4
  256.9 0.7 convolution_bitcast_fusion.5
  259.0 19.5 %fusion.4 = f32[1,4096]{1,0:T(1,128)S(1)} fusion(f32[2048,1]{0,1:T(1,128)S(1)} %bitcast.472, f32[1,2048,4096]{2,1,0:T(8,128)} %param.1), kind=kOutput, calls=%fused_computation.6 | convolution fusion | flops 100663296 | bytes 33579008 | tf_op jit(solution)/shard_map/mij,mi->mj/dot_general | solution.py:43
  278.5 13.2 %all-gather.10 = f32[16384]{0:T(1024)S(1)} all-gather(f32[4096]{0:T(1024)S(1)} %bitcast.467), channel_id=12, replica_groups=mesh['grp'=4,'section'=2,'row'=4] {'row'}, dimensions={0}, use_global_device_ids=true | all-gather | bytes 81920 | tf_op jit(solution)/shard_map/all_gather | solution.py:44
  291.7 2.0 all-gather.11
  293.8 0.6 multiply_reduce_fusion.4
  296.7 0.6 multiply_reduce_fusion.12
  298.0 0.6 multiply_reduce_fusion.11
  298.6 0.7 convolution_bitcast_fusion.2
  299.3 0.7 convolution_bitcast_fusion.3
  301.4 19.5 %fusion.2 = f32[1,4096]{1,0:T(1,128)S(1)} fusion(f32[2048,1]{0,1:T(1,128)S(1)} %bitcast.473, f32[1,2048,4096]{2,1,0:T(8,128)} %param.1), kind=kOutput, calls=%fused_computation.4 | convolution fusion | flops 100663296 | bytes 33579008 | tf_op jit(solution)/shard_map/mij,mi->mj/dot_general | solution.py:43
  320.9 13.2 %all-gather.12 = f32[16384]{0:T(1024)S(1)} all-gather(f32[4096]{0:T(1024)S(1)} %bitcast.468), channel_id=14, replica_groups=mesh['grp'=4,'section'=2,'row'=4] {'row'}, dimensions={0}, use_global_device_ids=true | all-gather | bytes 81920 | tf_op jit(solution)/shard_map/all_gather | solution.py:44
  334.2 2.1 all-gather.13
  339.3 0.6 multiply_reduce_fusion.10
  340.6 0.6 multiply_reduce_fusion.9
  341.2 0.7 convolution_bitcast_fusion
  341.9 0.7 convolution_bitcast_fusion.1
  344.0 19.5 %fusion = f32[1,4096]{1,0:T(1,128)S(1)} fusion(f32[2048,1]{0,1:T(1,128)S(1)} %bitcast.470, f32[1,2048,4096]{2,1,0:T(8,128)} %param.1), kind=kOutput, calls=%fused_computation.2 | convolution fusion | flops 100663296 | bytes 33579008 | tf_op jit(solution)/shard_map/mij,mi->mj/dot_general | solution.py:43
  363.9 13.2 %all-gather.14 = f32[16384]{0:T(1024)S(1)} all-gather(f32[4096]{0:T(1024)S(1)} %bitcast.462), channel_id=16, replica_groups=mesh['grp'=4,'section'=2,'row'=4] {'row'}, dimensions={0}, use_global_device_ids=true | all-gather | bytes 81920 | tf_op jit(solution)/shard_map/all_gather | solution.py:44
  377.1 2.1 all-gather.15
  380.9 30.3 %fusion.47 = f32[2048,4096]{1,0:T(8,128)} fusion(f32[1,8,8192]{2,1,0:T(8,128)S(1)} %stack.172, s32[]{:T(128)S(6)} %select_n.161, f32[1,8,8192]{2,1,0:T(8,128)S(1)} %stack.84, s32[]{:T(128)S(6)} %select_n.146), kind=kOutput, calls=%fused_computation.65 | convolution fusion | flops 805306368 | bytes 33751048 | tf_op jit(solution)/shard_map/mki,mkj->mij/dot_general | solution.py:63
  411.2 41.4 %bitcast_subtract_fusion = f32[1,2048,4096]{2,1,0:T(8,128)} fusion(f32[1,2048,4096]{2,1,0:T(8,128)} %param.1, f32[2048,4096]{1,0:T(8,128)} %fusion.47, f32[1,8,8192]{2,1,0:T(8,128)S(1)} %stack.84, s32[]{:T(128)S(6)} %select_n.161, f32[1,8,8192]{2,1,0:T(8,128)S(1)} %stack.172, s32[]{:T(128)S(6)} %select_n.146), kind=kOutput, calls=%fused_computation | convolution fusion | flops 822083584 | bytes 100859912 | tf_op jit(solution)/shard_map/mki,mkj->mij/dot_general | solution.py:64
  (88 shorter events, 17.5 us)
Async XLA Ops:
  6.5 23.6 %all-reduce.2.cloned.1.call-start = ((), (), s32[]{:S(2)}) async-start(), calls=%async_computation | async-start | bytes 131072 | tf_op jit(solution)/shard_map/psum | solution.py:12
Sparse Core Ops, SparseCore 0:
  9.6 20.4 all-reduce.1
